TPU v7x, 32 devices: a whole 2x2x4 slice. The times are simulated.
32 devices in a mesh: rows: 2 (over core), cols: 4 (over y, x), slabs: 4 (over z).
Axes of the slice: x: 2, y: 2, z: 4, core: 2. Of those that a mesh axis runs over, the one named last changes fastest.
Arguments:
- field_now: float32 [8, 128, 512, 128], P('rows', 'cols', 'slabs'), may hold values from 0.5 to 2
- earlier: float32 [8, 128, 512, 128], P('rows', 'cols', 'slabs'), may hold values from 0.2 to 1.8
- speed_square: float32 [8, 128, 512, 128], P('rows', 'cols', 'slabs'), may hold values from 0.05 to 0.3
Outputs:
- scaled_field: float32 [8, 128, 512, 128], P('rows', 'cols', 'slabs')
- field_now_end: float32 [8, 128, 512, 128], P('rows', 'cols', 'slabs')
All inputs are finite; a program needn't handle non-finite values.
Results may differ from a plain program's by a relative error of at most 0.00002.
Values sent between devices are 32-bit elements; how exact they have to be, the bound alone decides.
A program may use at most 128 MiB of HBM per device.

v0:
```python
import jax
import jax.numpy as jnp
from jax import lax
from jax.sharding import PartitionSpec as P

STEPS = 3


def with_halo(block, sides, width):
    for axis, dim in sides:
        count = lax.axis_size(axis)
        forward = [(i, i + 1) for i in range(count - 1)]
        backward = [(target, source) for source, target in forward]
        low = lax.ppermute(
            lax.slice_in_dim(block, block.shape[dim] - width, None, axis=dim), axis, forward
        )
        high = lax.ppermute(lax.slice_in_dim(block, 0, width, axis=dim), axis, backward)
        block = jnp.concatenate([low, block, high], axis=dim)
    return block


def without_rim(values, dims):
    for dim in dims:
        values = lax.slice_in_dim(values, 1, values.shape[dim] - 1, axis=dim)
    return values


def shifted_cells(values, dim, start, dims):
    others = [other for other in dims if other != dim]
    values = without_rim(values, others)
    return lax.slice_in_dim(values, start, start + values.shape[dim] - 2, axis=dim)


def march_step(padded, before, speed_square):
    middle = without_rim(padded, (0, 1, 2))
    lower = [shifted_cells(padded, dim, 0, (0, 1, 2)) for dim in (0, 1, 2)]
    upper = [shifted_cells(padded, dim, 2, (0, 1, 2)) for dim in (0, 1, 2)]
    spread = lower[0] + upper[0] + lower[1] + upper[1] + lower[2] + upper[2] - 6.0 * middle
    return 2.0 * middle - before + speed_square * spread


def shards(field_now, earlier, speed_square):
    for step in range(STEPS):
        padded = with_halo(field_now, (("rows", 0), ("cols", 1), ("slabs", 2)), 1)
        later = march_step(padded, earlier, speed_square)
        earlier, field_now = (field_now, later)
    count = field_now.shape[2] * lax.axis_size("slabs")
    guess = 1.0
    moved = field_now - guess
    totals, squares = lax.psum(
        (jnp.sum(moved, axis=2, keepdims=True), jnp.sum(moved * moved, axis=2, keepdims=True)),
        "slabs",
    )
    line_mean = guess + totals / count
    centred = field_now - line_mean
    line_variance = squares / count - totals / count * (totals / count)
    scaled_field = centred * lax.rsqrt(line_variance + 0.0001)
    return (scaled_field, field_now)


def solution(mesh):
    placed = (
        P("rows", "cols", "slabs", None),
        P("rows", "cols", "slabs", None),
        P("rows", "cols", "slabs", None),
    )
    return jax.shard_map(
        shards,
        mesh=mesh,
        in_specs=placed,
        out_specs=(P("rows", "cols", "slabs", None), P("rows", "cols", "slabs", None)),
        check_vma=False,
    )
```

profile of v0, /device:TPU:0, one launch (start us, length us, event | category | flops | bytes accessed | tf_op | source)
XLA Modules:
  0.0 269.9 jit_solution(9802183017727925755)
XLA Ops:
  7.2 4.1 %fusion.28 = (f32[1,32,128,128]{3,2,1,0:T(8,128)}, f32[1,32,128,128]{3,2,1,0:T(8,128)S(1)}) fusion(f32[4,32,128,128]{3,2,1,0:T(8,128)} %param.3), kind=kLoop, calls=%fused_computation.100 | loop fusion | bytes 8388608 | tf_op jit(solution)/shard_map/slice | solution.py:17
  11.3 2.6 collective-permute-start
  15.3 2.3 collective-permute-done
  17.6 1.3 copy-done.6
  20.4 1.7 constant_dynamic-update-slice_fusion
  22.2 4.2 %collective-permute-start.2 = (f32[6,1,128,128]{3,2,1,0:T(8,128)S(1)}, f32[6,1,128,128]{3,2,1,0:T(8,128)S(1)}, u32[]{:S(2)}, u32[]{:S(2)}) collective-permute-start(f32[6,1,128,128]{3,2,1,0:T(8,128)S(1)} %get-tuple-element.19), channel_id=1, source_target_pairs={{0,4},{4,8},{8,12},{1,5},{5,9},{9,13},{2,6},{6,10},{10,14},{3,7},{... | collective-permute-start | bytes 1179656 | tf_op jit(solution)/shard_map/ppermute | solution.py:14
  26.4 1.3 collective-permute-start.3
  27.7 7.5 %collective-permute-done.2 = f32[6,1,128,128]{3,2,1,0:T(8,128)S(1)} collective-permute-done((f32[6,1,128,128]{3,2,1,0:T(8,128)S(1)}, f32[6,1,128,128]{3,2,1,0:T(8,128)S(1)}, u32[]{:S(2)}, u32[]{:S(2)}) %collective-permute-start.2) | collective-permute-done | bytes 393248 | tf_op jit(solution)/shard_map/ppermute | solution.py:14
  35.2 10.4 %collective-permute-done.3 = f32[6,1,128,128]{3,2,1,0:T(8,128)S(1)} collective-permute-done((f32[6,1,128,128]{3,2,1,0:T(8,128)S(1)}, f32[6,1,128,128]{3,2,1,0:T(8,128)S(1)}, u32[]{:S(2)}, u32[]{:S(2)}) %collective-permute-start.3) | collective-permute-done | bytes 393248 | tf_op jit(solution)/shard_map/ppermute | solution.py:17
  47.0 4.6 %collective-permute-start.4 = (f32[6,34,1,128]{3,1,2,0:T(8,128)S(1)}, f32[6,34,1,128]{3,1,2,0:T(8,128)S(1)}, u32[]{:S(2)}, u32[]{:S(2)}) collective-permute-start(f32[6,34,1,128]{3,1,2,0:T(8,128)S(1)} %copy.19), channel_id=1, source_target_pairs={{0,1},{1,2},{2,3},{4,5},{5,6},{6,7},{8,9},{9,10},{10,11},{12,13},{... | collective-permute-start | bytes 313352 | tf_op jit(solution)/shard_map/ppermute | solution.py:14
  52.6 1.4 collective-permute-done.4
  54.1 27.4 %fusion.19 = f32[4,32,128,128]{3,2,1,0:T(8,128)S(1)} fusion(f32[4,32,128,128]{3,2,1,0:T(8,128)} %param.5, f32[6,34,1,128]{3,2,1,0:T(1,128)S(1)} %copy.22, f32[6,1,128,128]{3,2,1,0:T(8,128)S(1)} %collective-permute-done.3, f32[6,32,128,128]{3,2,1,0:T(8,128)} %copy-done.3, f32[6,1,128,128]{3,2,1,0:T(8,128)S(1)} %collective-permute-done.2, ...), kind=kLoop, calls=%fused_computation.56 | loop fusion | flops 44040192 | bytes 51326976 | tf_op jit(solution)/shard_map/add | solution.py:39
  82.1 1.4 collective-permute-start.6
  84.8 2.3 collective-permute-done.6
  87.2 2.4 collective-permute-done.7
  89.6 3.4 %collective-permute-start.8 = (f32[6,1,128,128]{3,2,1,0:T(8,128)S(1)}, f32[6,1,128,128]{3,2,1,0:T(8,128)S(1)}, u32[]{:S(2)}, u32[]{:S(2)}) collective-permute-start(f32[6,1,128,128]{3,2,1,0:T(8,128)S(1)} %get-tuple-element.17), channel_id=1, source_target_pairs={{0,4},{4,8},{8,12},{1,5},{5,9},{9,13},{2,6},{6,10},{10,14},{3,7},{... | collective-permute-start | bytes 1179656 | tf_op jit(solution)/shard_map/ppermute | solution.py:14
  94.4 7.3 %collective-permute-done.8 = f32[6,1,128,128]{3,2,1,0:T(8,128)S(1)} collective-permute-done((f32[6,1,128,128]{3,2,1,0:T(8,128)S(1)}, f32[6,1,128,128]{3,2,1,0:T(8,128)S(1)}, u32[]{:S(2)}, u32[]{:S(2)}) %collective-permute-start.8) | collective-permute-done | bytes 393248 | tf_op jit(solution)/shard_map/ppermute | solution.py:14
  101.7 9.2 %collective-permute-done.9 = f32[6,1,128,128]{3,2,1,0:T(8,128)S(1)} collective-permute-done((f32[6,1,128,128]{3,2,1,0:T(8,128)S(1)}, f32[6,1,128,128]{3,2,1,0:T(8,128)S(1)}, u32[]{:S(2)}, u32[]{:S(2)}) %collective-permute-start.9) | collective-permute-done | bytes 393248 | tf_op jit(solution)/shard_map/ppermute | solution.py:17
  112.4 5.0 %collective-permute-start.10 = (f32[6,34,1,128]{3,1,2,0:T(8,128)S(1)}, f32[6,34,1,128]{3,1,2,0:T(8,128)S(1)}, u32[]{:S(2)}, u32[]{:S(2)}) collective-permute-start(f32[6,34,1,128]{3,1,2,0:T(8,128)S(1)} %copy.23), channel_id=1, source_target_pairs={{0,1},{1,2},{2,3},{4,5},{5,6},{6,7},{8,9},{9,10},{10,11},{12,13},{... | collective-permute-start | bytes 313352 | tf_op jit(solution)/shard_map/ppermute | solution.py:14
  119.9 28.9 %fusion.11 = f32[4,32,128,128]{3,2,1,0:T(8,128)} fusion(f32[4,32,128,128]{3,2,1,0:T(8,128)} %param.5, f32[6,34,1,128]{3,2,1,0:T(1,128)S(1)} %copy.26, f32[6,1,128,128]{3,2,1,0:T(8,128)S(1)} %collective-permute-done.9, f32[6,1,128,128]{3,2,1,0:T(8,128)S(1)} %collective-permute-done.8, f32[1,32,128,128]{3,2,1,0:T(8,128)} %copy-done.5, ...), kind=kLoop, calls=%fused_computation.30 | loop fusion | flops 60817408 | bytes 38744064 | tf_op jit(solution)/shard_map/add | solution.py:39
  148.8 2.6 fusion.26
  151.4 1.7 collective-permute-start.12
  153.1 1.5 collective-permute-start.13
  154.6 2.2 collective-permute-done.12
  156.8 2.4 collective-permute-done.13
  159.2 1.5 collective-permute-start.14
  162.0 7.5 %collective-permute-done.14 = f32[6,1,128,128]{3,2,1,0:T(8,128)S(1)} collective-permute-done((f32[6,1,128,128]{3,2,1,0:T(8,128)S(1)}, f32[6,1,128,128]{3,2,1,0:T(8,128)S(1)}, u32[]{:S(2)}, u32[]{:S(2)}) %collective-permute-start.14) | collective-permute-done | bytes 393248 | tf_op jit(solution)/shard_map/ppermute | solution.py:14
  169.5 9.1 %collective-permute-done.15 = f32[6,1,128,128]{3,2,1,0:T(8,128)S(1)} collective-permute-done((f32[6,1,128,128]{3,2,1,0:T(8,128)S(1)}, f32[6,1,128,128]{3,2,1,0:T(8,128)S(1)}, u32[]{:S(2)}, u32[]{:S(2)}) %collective-permute-start.15) | collective-permute-done | bytes 393248 | tf_op jit(solution)/shard_map/ppermute | solution.py:17
  180.0 5.0 %collective-permute-start.16 = (f32[6,34,1,128]{3,1,2,0:T(8,128)S(1)}, f32[6,34,1,128]{3,1,2,0:T(8,128)S(1)}, u32[]{:S(2)}, u32[]{:S(2)}) collective-permute-start(f32[6,34,1,128]{3,1,2,0:T(8,128)S(1)} %copy.27), channel_id=1, source_target_pairs={{0,1},{1,2},{2,3},{4,5},{5,6},{6,7},{8,9},{9,10},{10,11},{12,13},{... | collective-permute-start | bytes 313352 | tf_op jit(solution)/shard_map/ppermute | solution.py:14
  187.5 29.8 %add_reduce_fusion = (f32[4,32,128]{2,1,0:T(8,128)}, f32[4,32,128]{2,1,0:T(8,128)}, f32[4,32,128,128]{3,2,1,0:T(8,128)}) fusion(f32[4,32,128,128]{3,2,1,0:T(8,128)} %param.5, f32[4,32,128,128]{3,2,1,0:T(8,128)} %fusion.11, f32[6,34,1,128]{3,2,1,0:T(1,128)S(1)} %copy.30, f32[6,1,128,128]{3,2,1,0:T(8,128)S(1)} %collective-permute-done.15, ...), kind=kLoop, calls=%fused_computation.72 | loop fusion | flops 69173248 | bytes 38875136 | tf_op jit(solution)/shard_map/reduce_sum | solution.py:51
  217.4 36.0 %all-reduce.3.cloned.1.call-done = (f32[4,32,1,128]{3,1,0,2:T(8,128)}, f32[4,32,1,128]{3,1,0,2:T(8,128)}) async-done(((f32[4,32,1,128]{3,1,0,2:T(8,128)}, f32[4,32,1,128]{3,1,0,2:T(8,128)}), (f32[4,32,1,128]{3,1,0,2:T(8,128)}, f32[4,32,1,128]{3,1,0,2:T(8,128)})) %all-reduce.3.cloned.1.call-update) | async-done | bytes 131088 | tf_op jit(solution)/shard_map/psum | solution.py:50
  254.2 8.8 %subtract_multiply_fusion = f32[4,32,128,128]{3,2,1,0:T(8,128)} fusion(f32[4,32,128,128]{3,2,1,0:T(8,128)} %get-tuple-element.8, f32[4,32,128]{2,1,0:T(8,128)S(1)} %get-tuple-element.28, f32[4,32,128]{2,1,0:T(8,128)S(1)} %get-tuple-element.27), kind=kLoop, calls=%fused_computation.71 | loop fusion | flops 4194304 | bytes 16908288 | tf_op jit(solution)/shard_map/mul | solution.py:57
  (50 shorter events, 18.8 us)
Async XLA Ops:
  7.2 246.2 %all-reduce.3.cloned.1.call-start = ((), (), s32[]{:S(2)}) async-start(), calls=%async_computation | async-start | bytes 262144 | tf_op jit(solution)/shard_map/psum | solution.py:50
  7.2 11.9 %copy-start.2 = (f32[4,32,128,128]{3,2,1,0:T(8,128)S(1)}, f32[4,32,128,128]{3,2,1,0:T(8,128)}, u32[]{:S(2)}) copy-start(f32[4,32,128,128]{3,2,1,0:T(8,128)} %param.3) | copy-start | bytes 25165828
  11.3 6.3 %collective-permute-start = (f32[1,32,128,128]{3,2,1,0:T(8,128)S(1)}, f32[1,32,128,128]{3,2,1,0:T(8,128)S(1)}, u32[]{:S(2)}, u32[]{:S(2)}) collective-permute-start(f32[1,32,128,128]{3,2,1,0:T(8,128)S(1)} %get-tuple-element.26), channel_id=1, source_target_pairs={{0,16},{1,17},{2,18},{3,19},{4,20},{5,21},{6,22},{7,23},{8,24},{9,... | collective-permute-start | bytes 6291464 | tf_op jit(solution)/shard_map/ppermute | solution.py:14
  14.0 6.4 %collective-permute-start.1 = (f32[1,32,128,128]{3,2,1,0:T(8,128)}, f32[1,32,128,128]{3,2,1,0:T(8,128)}, u32[]{:S(2)}, u32[]{:S(2)}) collective-permute-start(f32[1,32,128,128]{3,2,1,0:T(8,128)} %get-tuple-element.25), channel_id=1, source_target_pairs={{16,0},{17,1},{18,2},{19,3},{20,4},{21,5},{22,6},{23,7},{24,8},{25... | collective-permute-start | bytes 6291464 | tf_op jit(solution)/shard_map/ppermute | solution.py:17
  17.6 1.3 copy-start.6
  22.1 31.9 %copy-start.3 = (f32[6,32,128,128]{3,2,1,0:T(8,128)}, f32[6,32,128,128]{3,2,1,0:T(8,128)S(1)}, u32[]{:S(2)}) copy-start(f32[6,32,128,128]{3,2,1,0:T(8,128)S(1)} %constant_dynamic-update-slice_fusion) | copy-start | bytes 37748740
  22.2 13.0 %collective-permute-start.2 = (f32[6,1,128,128]{3,2,1,0:T(8,128)S(1)}, f32[6,1,128,128]{3,2,1,0:T(8,128)S(1)}, u32[]{:S(2)}, u32[]{:S(2)}) collective-permute-start(f32[6,1,128,128]{3,2,1,0:T(8,128)S(1)} %get-tuple-element.19), channel_id=1, source_target_pairs={{0,4},{4,8},{8,12},{1,5},{5,9},{9,13},{2,6},{6,10},{10,14},{3,7},{... | collective-permute-start | bytes 1179656 | tf_op jit(solution)/shard_map/ppermute | solution.py:14
  26.4 19.1 %collective-permute-start.3 = (f32[6,1,128,128]{3,2,1,0:T(8,128)S(1)}, f32[6,1,128,128]{3,2,1,0:T(8,128)S(1)}, u32[]{:S(2)}, u32[]{:S(2)}) collective-permute-start(f32[6,1,128,128]{3,2,1,0:T(8,128)S(1)} %get-tuple-element.20), channel_id=1, source_target_pairs={{4,0},{8,4},{12,8},{5,1},{9,5},{13,9},{6,2},{10,6},{14,10},{7,3},{... | collective-permute-start | bytes 1179656 | tf_op jit(solution)/shard_map/ppermute | solution.py:17
  45.7 6.8 %collective-permute-start.5 = (f32[6,34,1,128]{3,1,2,0:T(8,128)S(1)}, f32[6,34,1,128]{3,1,2,0:T(8,128)S(1)}, u32[]{:S(2)}, u32[]{:S(2)}) collective-permute-start(f32[6,34,1,128]{3,1,2,0:T(8,128)S(1)} %copy.21), channel_id=1, source_target_pairs={{1,0},{2,1},{3,2},{5,4},{6,5},{7,6},{9,8},{10,9},{11,10},{13,12},{... | collective-permute-start | bytes 313352 | tf_op jit(solution)/shard_map/ppermute | solution.py:17
  47.0 7.0 %collective-permute-start.4 = (f32[6,34,1,128]{3,1,2,0:T(8,128)S(1)}, f32[6,34,1,128]{3,1,2,0:T(8,128)S(1)}, u32[]{:S(2)}, u32[]{:S(2)}) collective-permute-start(f32[6,34,1,128]{3,1,2,0:T(8,128)S(1)} %copy.19), channel_id=1, source_target_pairs={{0,1},{1,2},{2,3},{4,5},{5,6},{6,7},{8,9},{9,10},{10,11},{12,13},{... | collective-permute-start | bytes 313352 | tf_op jit(solution)/shard_map/ppermute | solution.py:14
  81.6 29.3 %copy-start = (f32[4,32,128,128]{3,2,1,0:T(8,128)}, f32[4,32,128,128]{3,2,1,0:T(8,128)S(1)}, u32[]{:S(2)}) copy-start(f32[4,32,128,128]{3,2,1,0:T(8,128)S(1)} %fusion.19) | copy-start | bytes 25165828
  82.1 5.1 %collective-permute-start.6 = (f32[1,32,128,128]{3,2,1,0:T(8,128)S(1)}, f32[1,32,128,128]{3,2,1,0:T(8,128)S(1)}, u32[]{:S(2)}, u32[]{:S(2)}) collective-permute-start(f32[1,32,128,128]{3,2,1,0:T(8,128)S(1)} %get-tuple-element.23), channel_id=1, source_target_pairs={{0,16},{1,17},{2,18},{3,19},{4,20},{5,21},{6,22},{7,23},{8,24},{9,... | collective-permute-start | bytes 6291464 | tf_op jit(solution)/shard_map/ppermute | solution.py:14
  83.5 6.1 %collective-permute-start.7 = (f32[1,32,128,128]{3,2,1,0:T(8,128)S(1)}, f32[1,32,128,128]{3,2,1,0:T(8,128)S(1)}, u32[]{:S(2)}, u32[]{:S(2)}) collective-permute-start(f32[1,32,128,128]{3,2,1,0:T(8,128)S(1)} %get-tuple-element.24), channel_id=1, source_target_pairs={{16,0},{17,1},{18,2},{19,3},{20,4},{21,5},{22,6},{23,7},{24,8},{25... | collective-permute-start | bytes 6291464 | tf_op jit(solution)/shard_map/ppermute | solution.py:17
  89.6 21.5 %copy-start.5 = (f32[1,32,128,128]{3,2,1,0:T(8,128)}, f32[1,32,128,128]{3,2,1,0:T(8,128)S(1)}, u32[]{:S(2)}) copy-start(f32[1,32,128,128]{3,2,1,0:T(8,128)S(1)} %collective-permute-done.7) | copy-start | bytes 6291460
  89.6 12.1 %collective-permute-start.8 = (f32[6,1,128,128]{3,2,1,0:T(8,128)S(1)}, f32[6,1,128,128]{3,2,1,0:T(8,128)S(1)}, u32[]{:S(2)}, u32[]{:S(2)}) collective-permute-start(f32[6,1,128,128]{3,2,1,0:T(8,128)S(1)} %get-tuple-element.17), channel_id=1, source_target_pairs={{0,4},{4,8},{8,12},{1,5},{5,9},{9,13},{2,6},{6,10},{10,14},{3,7},{... | collective-permute-start | bytes 1179656 | tf_op jit(solution)/shard_map/ppermute | solution.py:14
  93.1 17.8 %collective-permute-start.9 = (f32[6,1,128,128]{3,2,1,0:T(8,128)S(1)}, f32[6,1,128,128]{3,2,1,0:T(8,128)S(1)}, u32[]{:S(2)}, u32[]{:S(2)}) collective-permute-start(f32[6,1,128,128]{3,2,1,0:T(8,128)S(1)} %get-tuple-element.18), channel_id=1, source_target_pairs={{4,0},{8,4},{12,8},{5,1},{9,5},{13,9},{6,2},{10,6},{14,10},{7,3},{... | collective-permute-start | bytes 1179656 | tf_op jit(solution)/shard_map/ppermute | solution.py:17
  111.1 7.4 %collective-permute-start.11 = (f32[6,34,1,128]{3,1,2,0:T(8,128)S(1)}, f32[6,34,1,128]{3,1,2,0:T(8,128)S(1)}, u32[]{:S(2)}, u32[]{:S(2)}) collective-permute-start(f32[6,34,1,128]{3,1,2,0:T(8,128)S(1)} %copy.25), channel_id=1, source_target_pairs={{1,0},{2,1},{3,2},{5,4},{6,5},{7,6},{9,8},{10,9},{11,10},{13,12},{... | collective-permute-start | bytes 313352 | tf_op jit(solution)/shard_map/ppermute | solution.py:17
  112.4 7.4 %collective-permute-start.10 = (f32[6,34,1,128]{3,1,2,0:T(8,128)S(1)}, f32[6,34,1,128]{3,1,2,0:T(8,128)S(1)}, u32[]{:S(2)}, u32[]{:S(2)}) collective-permute-start(f32[6,34,1,128]{3,1,2,0:T(8,128)S(1)} %copy.23), channel_id=1, source_target_pairs={{0,1},{1,2},{2,3},{4,5},{5,6},{6,7},{8,9},{9,10},{10,11},{12,13},{... | collective-permute-start | bytes 313352 | tf_op jit(solution)/shard_map/ppermute | solution.py:14
  148.8 10.4 %copy-start.1 = (f32[4,32,128,128]{3,2,1,0:T(8,128)S(1)}, f32[4,32,128,128]{3,2,1,0:T(8,128)}, u32[]{:S(2)}) copy-start(f32[4,32,128,128]{3,2,1,0:T(8,128)} %fusion.11) | copy-start | bytes 25165828
  151.4 5.3 %collective-permute-start.12 = (f32[1,32,128,128]{3,2,1,0:T(8,128)S(1)}, f32[1,32,128,128]{3,2,1,0:T(8,128)S(1)}, u32[]{:S(2)}, u32[]{:S(2)}) collective-permute-start(f32[1,32,128,128]{3,2,1,0:T(8,128)S(1)} %get-tuple-element.21), channel_id=1, source_target_pairs={{0,16},{1,17},{2,18},{3,19},{4,20},{5,21},{6,22},{7,23},{8,24},{9,... | collective-permute-start | bytes 6291464 | tf_op jit(solution)/shard_map/ppermute | solution.py:14
  153.1 6.1 %collective-permute-start.13 = (f32[1,32,128,128]{3,2,1,0:T(8,128)S(1)}, f32[1,32,128,128]{3,2,1,0:T(8,128)S(1)}, u32[]{:S(2)}, u32[]{:S(2)}) collective-permute-start(f32[1,32,128,128]{3,2,1,0:T(8,128)S(1)} %get-tuple-element.22), channel_id=1, source_target_pairs={{16,0},{17,1},{18,2},{19,3},{20,4},{21,5},{22,6},{23,7},{24,8},{25... | collective-permute-start | bytes 6291464 | tf_op jit(solution)/shard_map/ppermute | solution.py:17
  159.2 19.5 %copy-start.4 = (f32[1,32,128,128]{3,2,1,0:T(8,128)}, f32[1,32,128,128]{3,2,1,0:T(8,128)S(1)}, u32[]{:S(2)}) copy-start(f32[1,32,128,128]{3,2,1,0:T(8,128)S(1)} %collective-permute-done.13) | copy-start | bytes 6291460
  159.2 10.2 %collective-permute-start.14 = (f32[6,1,128,128]{3,2,1,0:T(8,128)S(1)}, f32[6,1,128,128]{3,2,1,0:T(8,128)S(1)}, u32[]{:S(2)}, u32[]{:S(2)}) collective-permute-start(f32[6,1,128,128]{3,2,1,0:T(8,128)S(1)} %get-tuple-element.15), channel_id=1, source_target_pairs={{0,4},{4,8},{8,12},{1,5},{5,9},{9,13},{2,6},{6,10},{10,14},{3,7},{... | collective-permute-start | bytes 1179656 | tf_op jit(solution)/shard_map/ppermute | solution.py:14
  160.7 17.8 %collective-permute-start.15 = (f32[6,1,128,128]{3,2,1,0:T(8,128)S(1)}, f32[6,1,128,128]{3,2,1,0:T(8,128)S(1)}, u32[]{:S(2)}, u32[]{:S(2)}) collective-permute-start(f32[6,1,128,128]{3,2,1,0:T(8,128)S(1)} %get-tuple-element.16), channel_id=1, source_target_pairs={{4,0},{8,4},{12,8},{5,1},{9,5},{13,9},{6,2},{10,6},{14,10},{7,3},{... | collective-permute-start | bytes 1179656 | tf_op jit(solution)/shard_map/ppermute | solution.py:17
  178.7 7.4 %collective-permute-start.17 = (f32[6,34,1,128]{3,1,2,0:T(8,128)S(1)}, f32[6,34,1,128]{3,1,2,0:T(8,128)S(1)}, u32[]{:S(2)}, u32[]{:S(2)}) collective-permute-start(f32[6,34,1,128]{3,1,2,0:T(8,128)S(1)} %copy.29), channel_id=1, source_target_pairs={{1,0},{2,1},{3,2},{5,4},{6,5},{7,6},{9,8},{10,9},{11,10},{13,12},{... | collective-permute-start | bytes 313352 | tf_op jit(solution)/shard_map/ppermute | solution.py:17
  180.0 7.4 %collective-permute-start.16 = (f32[6,34,1,128]{3,1,2,0:T(8,128)S(1)}, f32[6,34,1,128]{3,1,2,0:T(8,128)S(1)}, u32[]{:S(2)}, u32[]{:S(2)}) collective-permute-start(f32[6,34,1,128]{3,1,2,0:T(8,128)S(1)} %copy.27), channel_id=1, source_target_pairs={{0,1},{1,2},{2,3},{4,5},{5,6},{6,7},{8,9},{9,10},{10,11},{12,13},{... | collective-permute-start | bytes 313352 | tf_op jit(solution)/shard_map/ppermute | solution.py:14
Sparse Core Ops, SparseCore 0:
  217.5 35.7 all-reduce.2
where the time goes:
time: 271 us; the launch traced here: 270 us
  waiting for transfers between devices  106 us (39%)
  other arithmetic  96.4 us (36%)
  starting transfers between devices  41.2 us (15%)
  between operations  14.4 us (5%)
  local copies, waits for them, and re-layouts  12.4 us (5%)
    add x2, other arithmetic, march_step(): return 2.0 * middle - before + speed_square * spread  56.3 us
    ppermute x9, waiting for transfers between devices, with_halo(): lax.ppermute(lax.slice_in_dim(block, 0, width, axis=dim), axis, backward)  36.6 us
    psum x1, waiting for transfers between devices, shards(): lax.psum((jnp.sum(moved, axis=2, keepdims=True), jnp.sum(moved * moved, a...  36 us
    ppermute x9, waiting for transfers between devices, with_halo(): lax.ppermute(lax.slice_in_dim(block, block.shape[dim] - width, None, axis...  32.9 us
    reduce_sum x1, other arithmetic, shards(): jnp.sum(moved, axis=2, keepdims=True)  29.8 us
    ppermute x9, starting transfers between devices, with_halo(): lax.ppermute(lax.slice_in_dim(block, block.shape[dim] - width, None, axis...  29.4 us
    ppermute x9, starting transfers between devices, with_halo(): lax.ppermute(lax.slice_in_dim(block, 0, width, axis=dim), axis, backward)  11.8 us
    mul x1, other arithmetic, shards(): scaled_field = centred * lax.rsqrt(line_variance + 0.0001)  8.85 us
  transfers between devices with their start and end apart: 19, of which 19 were waited for; matrix products, arithmetic and copies ran while one was open for 1% of the time, Pallas kernels for 0%

commit v1 on v0

v1 whole, which is shorter than its diff:
```python
import functools

import jax
import jax.numpy as jnp
from jax import lax
from jax.experimental import pallas as pl
from jax.experimental.pallas import tpu as pltpu
from jax.sharding import PartitionSpec as P

STEPS = 3
EPS = 1e-4
MESH = pl.DeviceIdType.MESH
AXES = ("rows", "cols", "slabs")


def march_kernel(
    counts, relay, now_hbm, old_hbm, speed_hbm, field, mean_ref, scale_ref,
    work, speed, face_out, face_in, own_stats, own_edge, in_stats, all_edge,
    relayed, load_x, load_y, load_c, send_sem, recv_sem, half_send, half_recv,
    pass_send, pass_recv, stat_send, stat_recv, edge_send, edge_recv,
):
    nj, ni, nk, lanes = now_hbm.shape
    n_slabs = counts["slabs"]
    parts = speed_parts(ni)
    width = ni // parts
    here = {axis: lax.axis_index(axis) for axis in AXES}
    has_low = {axis: here[axis] > 0 for axis in AXES}
    has_high = {axis: here[axis] < counts[axis] - 1 for axis in AXES}

    inner = (pl.ds(1, nj), pl.ds(1, ni))
    copy_x = pltpu.make_async_copy(now_hbm, work.at[inner], load_x)
    copy_x.start()
    copies = []
    for part in range(parts):
        span, padded = pl.ds(part * width, width), pl.ds(1 + part * width, width)
        copies.append((
            pltpu.make_async_copy(old_hbm.at[:, span], field.at[pl.ds(1, nj), padded], load_y.at[part]),
            pltpu.make_async_copy(speed_hbm.at[:, span], speed.at[:, span], load_c.at[part]),
        ))
        for copy in copies[-1]:
            copy.start()

    barrier = pltpu.get_barrier_semaphore()
    expected = jnp.int32(n_slabs - 1)
    for axis in ("rows", "cols"):
        for there, shift in ((has_low[axis], -1), (has_high[axis], 1)):
            expected = expected + there.astype(jnp.int32)

            @pl.when(there)
            def _():
                pl.semaphore_signal(barrier, inc=1, device_id={axis: here[axis] + shift}, device_id_type=MESH)

    peers = [lax.rem(here["slabs"] + gap, n_slabs) for gap in range(1, n_slabs)]
    for peer in peers:
        pl.semaphore_signal(barrier, inc=1, device_id={"slabs": peer}, device_id_type=MESH)
    if relay:
        over = lax.rem(here["cols"] + 2, 4)
        pl.semaphore_signal(barrier, inc=1, device_id={"cols": over}, device_id_type=MESH)
        expected = expected + 1
    pl.semaphore_wait(barrier, expected)

    half = nj // 2 if relay else 0

    def half_copy(step, to_high, kind):
        buffer = work if step % 2 == 0 else field
        edge = ni - 1 if to_high else 0
        source = now_hbm.at[pl.ds(0, half), edge] if step == 0 else buffer.at[pl.ds(1, half), edge + 1]
        landing = buffer.at[pl.ds(1, half), 0 if to_high else ni + 1]
        sems = half_send.at[step, int(to_high)], half_recv.at[step, int(to_high)]
        target = here["cols"] + (1 if to_high else -1)
        if kind == "to":
            landing, target = relayed.at[step], over
            sems = sems[0], pass_recv.at[step]
        elif kind == "on":
            source, target = relayed.at[step], here["cols"] + (-1 if to_high else 1)
            sems = pass_send.at[step], sems[1]
        return pltpu.make_async_remote_copy(
            source, landing, *sems, device_id={"cols": target}, device_id_type=MESH
        )

    def halves(step, what):
        if not relay:
            return
        me = here["cols"]
        for to_high, source, target in ((True, 1, 2), (False, 2, 1)):
            edge_sends = (me == 0) | (me == 2) if to_high else (me == 1) | (me == 3)
            if what == "start":
                pl.when(me == source)(half_copy(step, to_high, "to").start)
                pl.when(edge_sends)(half_copy(step, to_high, "straight").start)
            elif what == "pass":
                @pl.when(me == (3 if to_high else 0))
                def _():
                    half_copy(step, to_high, "to").wait_recv()
                    half_copy(step, to_high, "on").start()
            elif what == "sent":
                pl.when(has_high["cols"] if to_high else has_low["cols"])(
                    half_copy(step, to_high, "straight").wait_send
                )
                pl.when(me == (3 if to_high else 0))(half_copy(step, to_high, "on").wait_send)
            else:
                pl.when(has_low["cols"] if to_high else has_high["cols"])(
                    half_copy(step, to_high, "straight").wait_recv
                )

    def face_copy(step, axis, to_high):
        buffer = work if step % 2 == 0 else field
        number = 2 * AXES.index(axis) + int(to_high)
        target = here[axis] + (1 if to_high else -1)
        if axis == "slabs":
            source, landing = face_out.at[step, int(to_high)], face_in.at[step, int(to_high)]
        elif axis == "cols":
            edge = ni - 1 if to_high else 0
            rest = pl.ds(half, nj - half)
            source = now_hbm.at[rest, edge] if step == 0 else buffer.at[pl.ds(1 + half, nj - half), edge + 1]
            landing = buffer.at[pl.ds(1 + half, nj - half), 0 if to_high else ni + 1]
        else:
            edge = nj - 1 if to_high else 0
            source = now_hbm.at[edge] if step == 0 else buffer.at[edge + 1, pl.ds(1, ni)]
            landing = buffer.at[0 if to_high else nj + 1, pl.ds(1, ni)]
        return pltpu.make_async_remote_copy(
            source, landing, send_sem.at[step, number], recv_sem.at[step, number],
            device_id={axis: target}, device_id_type=MESH,
        )

    def exchange(step, axis, what):
        if axis == "cols":
            halves(step, what)
        for to_high in (False, True):
            sends = has_high[axis] if to_high else has_low[axis]
            takes = has_low[axis] if to_high else has_high[axis]
            copy = face_copy(step, axis, to_high)
            if what == "start":
                pl.when(sends)(copy.start)
            elif what == "sent":
                pl.when(sends)(copy.wait_send)
            else:
                pl.when(takes)(copy.wait_recv)

    exchange(0, "cols", "start")
    exchange(0, "rows", "start")

    zeros_line = jnp.zeros((nk, lanes), jnp.float32)
    for buffer in (work, field):
        for absent, edge in ((~has_low["rows"], 0), (~has_high["rows"], nj + 1)):
            @pl.when(absent)
            def _():
                @pl.loop(1, ni + 1)
                def _(i):
                    buffer[edge, i] = zeros_line
        for absent, edge in ((~has_low["cols"], 0), (~has_high["cols"], ni + 1)):
            @pl.when(absent)
            def _():
                @pl.loop(1, nj + 1)
                def _(j):
                    buffer[j, edge] = zeros_line
    for absent, side in ((~has_low["slabs"], 1), (~has_high["slabs"], 0)):
        @pl.when(absent)
        def _():
            for step in range(STEPS):
                face_in[step, side] = jnp.zeros((nj, ni, lanes), jnp.float32)
    own_stats[...] = jnp.zeros_like(own_stats)

    copy_x.wait()

    @pl.loop(0, ni)
    def _(i):
        for j in range(nj):
            face_out[0, 0, j, pl.ds(i, 1), :] = work[j + 1, i + 1, pl.ds(0, 1), :]
            face_out[0, 1, j, pl.ds(i, 1), :] = work[j + 1, i + 1, pl.ds(nk - 1, 1), :]

    exchange(0, "slabs", "start")

    groups = nk // 8
    row_number = lax.broadcasted_iota(jnp.int32, (8, lanes), 0)

    def line(step, i, edge_side=None):
        now, old = (work, field) if step % 2 == 1 else (field, work)
        last = step == STEPS
        sums = [None] * nj
        for g in range(groups):
            k = pl.ds(8 * g, 8)
            column = [now[j, i, k, :] for j in range(nj + 2)]
            for j in range(1, nj + 1):
                middle = column[j]
                if g == 0:
                    low = jnp.where(
                        row_number == 0,
                        jnp.broadcast_to(face_in[step - 1, 1, j - 1, pl.ds(i - 1, 1), :], (8, lanes)),
                        pltpu.roll(middle, 1, 0),
                    )
                else:
                    low = now[j, i, pl.ds(8 * g - 1, 8), :]
                if g == groups - 1:
                    high = jnp.where(
                        row_number == 7,
                        jnp.broadcast_to(face_in[step - 1, 0, j - 1, pl.ds(i - 1, 1), :], (8, lanes)),
                        pltpu.roll(middle, 7, 0),
                    )
                else:
                    high = now[j, i, pl.ds(8 * g + 1, 8), :]
                spread = (
                    (column[j - 1] + column[j + 1])
                    + (now[j, i - 1, k, :] + now[j, i + 1, k, :])
                    + (low + high)
                    - 6.0 * middle
                )
                later = 2.0 * middle - old[j, i, k, :] + speed[j - 1, i - 1, k, :] * spread
                old[j, i, k, :] = later
                if last:
                    sums[j - 1] = later if g == 0 else sums[j - 1] + later
                else:
                    if g == 0:
                        face_out[step, 0, j - 1, pl.ds(i - 1, 1), :] = later[0:1]
                    if g == groups - 1:
                        face_out[step, 1, j - 1, pl.ds(i - 1, 1), :] = later[7:8]
        if last:
            for j in range(nj):
                total = jnp.sum(sums[j], axis=0, keepdims=True)
                mean = jnp.broadcast_to(total * (1.0 / nk), (8, lanes))
                squares = None
                for g in range(groups):
                    moved = old[j + 1, i, pl.ds(8 * g, 8), :] - mean
                    squares = moved * moved if g == 0 else squares + moved * moved
                square = jnp.sum(squares, axis=0, keepdims=True)
                if edge_side is None:
                    own_stats[0, 0, j, pl.ds(i - 1, 1), :] = total
                    own_stats[0, 1, j, pl.ds(i - 1, 1), :] = square
                else:
                    own_edge[0, pl.ds(edge_side * nj + j, 1), :] = total
                    own_edge[1, pl.ds(edge_side * nj + j, 1), :] = square

    def lines(step, start, stop):
        @pl.loop(start, stop)
        def _(i):
            line(step, i)

    levels = n_slabs.bit_length() - 1
    partners = []
    for level in range(levels):
        bit = lax.rem(here["slabs"] // 2**level, 2)
        partners.append(here["slabs"] + (1 - 2 * bit) * 2**level)

    def stat_copy(part, level):
        rows = pl.ds(part * width, width)
        return pltpu.make_async_remote_copy(
            own_stats.at[level, :, :, rows], in_stats.at[level, :, :, rows],
            stat_send.at[part, level], stat_recv.at[part, level],
            device_id={"slabs": partners[level]}, device_id_type=MESH,
        )

    def edge_copy(gap):
        return pltpu.make_async_remote_copy(
            own_edge, all_edge.at[gap - 1], edge_send.at[gap - 1], edge_recv.at[gap - 1],
            device_id={"slabs": peers[gap - 1]}, device_id_type=MESH,
        )

    def merged(part, level):
        rows = pl.ds(part * width, width)
        stat_copy(part, level).wait_recv()
        mine, theirs = own_stats[level, :, :, rows, :], in_stats[level, :, :, rows, :]
        cells = float(nk * 2**level)
        apart = (theirs[0] - mine[0]) * (1.0 / cells)
        return mine[0] + theirs[0], mine[1] + theirs[1] + (0.5 * cells) * apart * apart

    def advance(part, level):
        rows = pl.ds(part * width, width)
        total, square = merged(part, level)
        own_stats[level + 1, 0, :, rows, :] = total
        own_stats[level + 1, 1, :, rows, :] = square
        stat_copy(part, level + 1).start()

    gaps = range(1, n_slabs)
    for step in range(1, STEPS + 1):
        if step == 3:
            for axis in AXES:
                exchange(1, axis, "sent")
        exchange(step - 1, "rows", "taken")
        exchange(step - 1, "slabs", "taken")
        for part in range(parts):
            if step == 1:
                for copy in copies[part]:
                    copy.wait()
            start, stop = 1 + part * width, 1 + (part + 1) * width
            lines(step, max(start, 2), min(stop, ni))
            if part == 0:
                halves(step - 1, "pass")
            if step == STEPS:
                stat_copy(part, 0).start()
                if part >= 2 and levels > 1:
                    advance(part - 2, 0)
        if step == STEPS and levels > 1:
            for part in range(max(parts - 2, 0), parts):
                advance(part, 0)
        exchange(step - 1, "cols", "taken")
        line(step, 1, 0)
        line(step, ni, 1)
        if step < STEPS:
            for axis in ("cols", "slabs", "rows"):
                exchange(step, axis, "start")
    for gap in gaps:
        edge_copy(gap).start()
    for level in range(1, levels - 1):
        for part in range(parts):
            advance(part, level)

    whole = float(nk * n_slabs)

    def combine(own, others):
        mean = own[0]
        for other in others:
            mean = mean + other[0]
        mean = mean * (1.0 / whole)
        square = None
        for one in (own, *others):
            gap = one[0] * (1.0 / nk) - mean
            term = one[1] + nk * gap * gap
            square = term if square is None else square + term
        return mean, lax.rsqrt(square * (1.0 / whole) + EPS)

    for part in range(parts):
        rows = pl.ds(part * width, width)
        total, square = merged(part, levels - 1)
        mean_ref[:, rows, :] = total * (1.0 / whole)
        scale_ref[:, rows, :] = lax.rsqrt(square * (1.0 / whole) + EPS)
    for gap in gaps:
        edge_copy(gap).wait_recv()
    mean, scale = combine(own_edge[...], [all_edge[gap - 1] for gap in gaps])
    for side, i in ((0, 0), (1, ni - 1)):
        for j in range(nj):
            place = side * nj + j
            mean_ref[j, pl.ds(i, 1), :] = mean[place:place + 1]
            scale_ref[j, pl.ds(i, 1), :] = scale[place:place + 1]

    for step in range(STEPS):
        if step != 1:
            for axis in AXES:
                exchange(step, axis, "sent")
    for part in range(parts):
        for level in range(levels):
            stat_copy(part, level).wait_send()
    for gap in gaps:
        edge_copy(gap).wait_send()


def speed_parts(ni):
    return 4 if ni % 32 == 0 else 1


def scale_kernel(field, mean_ref, scale_ref, scaled_hbm, field_hbm, scaled, out_sem, field_sem):
    nj, ni, nk, lanes = scaled_hbm.shape
    parts = speed_parts(ni)
    width = ni // parts
    field_copies = [
        pltpu.make_async_copy(field.at[j + 1, pl.ds(1, ni)], field_hbm.at[j], field_sem.at[j])
        for j in range(nj)
    ]
    out_copies = []
    for j in range(nj):
        for part in range(parts):
            @pl.loop(part * width, (part + 1) * width)
            def _(i):
                mean = jnp.broadcast_to(mean_ref[j, pl.ds(i, 1), :], (8, lanes))
                scale = jnp.broadcast_to(scale_ref[j, pl.ds(i, 1), :], (8, lanes))
                for g in range(nk // 8):
                    k = pl.ds(8 * g, 8)
                    scaled[j, i, k, :] = (field[j + 1, i + 1, k, :] - mean) * scale

            rows = pl.ds(part * width, width)
            copy = pltpu.make_async_copy(
                scaled.at[j, rows], scaled_hbm.at[j, rows], out_sem.at[j, part]
            )
            copy.start()
            out_copies.append(copy)
            if part == 0:
                field_copies[j].start()
    for copy in (*field_copies, *out_copies):
        copy.wait()


def shards(counts, relay, field_now, earlier, speed_square):
    nj, ni, nk, lanes = field_now.shape
    n_slabs = counts["slabs"]
    levels = n_slabs.bit_length() - 1
    assert n_slabs == 2**levels and levels >= 1
    relay = relay and nj > 1
    parts = speed_parts(ni)
    f32 = jnp.float32
    padded = (nj + 2, ni + 2, nk, lanes)
    hbm = pl.BlockSpec(memory_space=pltpu.HBM)
    vmem = pl.BlockSpec(memory_space=pltpu.VMEM)
    cells = nj * ni * nk * lanes
    dma = pltpu.SemaphoreType.DMA
    field, mean, scale = pl.pallas_call(
        functools.partial(march_kernel, counts, relay),
        name="march",
        out_shape=(
            pltpu.VMEM(padded, f32),
            pltpu.VMEM((nj, ni, lanes), f32),
            pltpu.VMEM((nj, ni, lanes), f32),
        ),
        in_specs=[hbm] * 3,
        out_specs=(vmem,) * 3,
        scratch_shapes=[
            pltpu.VMEM(padded, f32),
            pltpu.VMEM((nj, ni, nk, lanes), f32),
            pltpu.VMEM((STEPS, 2, nj, ni, lanes), f32),
            pltpu.VMEM((STEPS, 2, nj, ni, lanes), f32),
            pltpu.VMEM((levels, 2, nj, ni, lanes), f32),
            pltpu.VMEM((2, 2 * nj, lanes), f32),
            pltpu.VMEM((levels, 2, nj, ni, lanes), f32),
            pltpu.VMEM((n_slabs - 1, 2, 2 * nj, lanes), f32),
            pltpu.VMEM((STEPS, max(nj // 2, 1), nk, lanes), f32),
            dma(()),
            dma((parts,)),
            dma((parts,)),
            dma((STEPS, 6)),
            dma((STEPS, 6)),
            dma((STEPS, 2)),
            dma((STEPS, 2)),
            dma((STEPS,)),
            dma((STEPS,)),
            dma((parts, levels)),
            dma((parts, levels)),
            dma((n_slabs - 1,)),
            dma((n_slabs - 1,)),
        ],
        compiler_params=pltpu.CompilerParams(
            collective_id=0, has_side_effects=True, vmem_limit_bytes=45 * 2**20
        ),
        cost_estimate=pl.CostEstimate(flops=33 * cells, bytes_accessed=12 * cells, transcendentals=0),
    )(field_now, earlier, speed_square)
    return pl.pallas_call(
        scale_kernel,
        name="scale",
        out_shape=(jax.ShapeDtypeStruct(field_now.shape, f32),) * 2,
        in_specs=[vmem] * 3,
        out_specs=(hbm,) * 2,
        scratch_shapes=[
            pltpu.VMEM((nj, ni, nk, lanes), f32),
            dma((nj, parts)),
            dma((nj,)),
        ],
        compiler_params=pltpu.CompilerParams(vmem_limit_bytes=16 * 2**20),
        cost_estimate=pl.CostEstimate(flops=2 * cells, bytes_accessed=8 * cells, transcendentals=0),
    )(field, mean, scale)


def crosses(mesh):
    order = ("rows", "cols", "slabs")
    devices = mesh.devices.transpose([mesh.axis_names.index(axis) for axis in order])
    if devices.shape[1] != 4:
        return False
    one, other = (getattr(devices[0, place, 0], "coords", None) for place in (1, 2))
    return one is not None and sum(a != b for a, b in zip(one, other)) > 1


def solution(mesh):
    spec = P("rows", "cols", "slabs", None)
    return jax.shard_map(
        functools.partial(shards, dict(mesh.shape), crosses(mesh)),
        mesh=mesh,
        in_specs=(spec,) * 3,
        out_specs=(spec,) * 2,
        check_vma=False,
    )
```

time: 271 us -> 51.8 us (0.19)
  waiting for transfers between devices: 106 us -> 0 us
  other arithmetic: 96.4 us -> 0 us
  Pallas kernels: 0 us -> 51 us
  starting transfers between devices: 41.2 us -> 0 us
  between operations: 14.4 us -> 0.64 us
  local copies, waits for them, and re-layouts: 12.4 us -> 0 us
    ppermute x18 -> x0, waiting for transfers between devices: 69.5 us -> none  [the longest x9 36.6 us: with_halo(): lax.ppermute(lax.slice_in_dim(block, 0, width, axis=dim), axis, backward)]
    add x2 -> x0, other arithmetic: 56.3 us -> none  [march_step(): return 2.0 * middle - before + speed_square * spread]
    pallas_call x0 -> x2, Pallas kernels: none -> 51 us  [the longest x1 45 us: shards(): pl.pallas_call(functools.partial(march_kernel, counts, relay), name='marc...]
    ppermute x18 -> x0, starting transfers between devices: 41.2 us -> none  [the longest x9 29.4 us: with_halo(): lax.ppermute(lax.slice_in_dim(block, block.shape[dim] - width, None, axis...]
    psum x1 -> x0, waiting for transfers between devices: 36 us -> none  [shards(): lax.psum((jnp.sum(moved, axis=2, keepdims=True), jnp.sum(moved * moved, a...]
    reduce_sum x1 -> x0, other arithmetic: 29.8 us -> none  [shards(): jnp.sum(moved, axis=2, keepdims=True)]
    mul x1 -> x0, other arithmetic: 8.85 us -> none  [shards(): scaled_field = centred * lax.rsqrt(line_variance + 0.0001)]
    slice x10 -> x0, local copies, waits for them, and re-layouts: 7.32 us -> none  [the longest x4 4.11 us: with_halo(): lax.slice_in_dim(block, 0, width, axis=dim)]
  transfers between devices with their start and end apart: 19 -> 0, of which waited for: 19 -> 0; matrix products, arithmetic and copies ran while one was open for 1% -> 0% of each run, Pallas kernels for 0% -> 0%
where the time goes in v1:
time: 51.8 us; the launch traced here: 51.7 us
  Pallas kernels  51 us (98%)
  between operations  0.64 us (1%)
    pallas_call x1, Pallas kernels, shards(): pl.pallas_call(functools.partial(march_kernel, counts, relay), name='marc...  45 us
    pallas_call x1, Pallas kernels, shards(): pl.pallas_call(scale_kernel, name='scale', out_shape=(jax.ShapeDtypeStruc...  6.04 us

profile of v1, /device:TPU:0, one launch (start us, length us, event | category | flops | bytes accessed | tf_op | source)
XLA Modules:
  0.0 51.7 jit_solution(8737286688752405201)
XLA Ops:
  0.6 45.0 %march.1 = (f32[6,34,128,128]{3,2,1,0:T(8,128)S(1)}, f32[4,32,128]{2,1,0:T(8,128)S(1)}, f32[4,32,128]{2,1,0:T(8,128)S(1)}) custom-call(f32[4,32,128,128]{3,2,1,0:T(8,128)} %now_hbm.1, f32[4,32,128,128]{3,2,1,0:T(8,128)} %old_hbm.1, f32[4,32,128,128]{3,2,1,0:T(8,128)} %speed_hbm.1), custom_call_target="tpu_custom_call" | custom-call | flops 69206016 | bytes 25165824 | tf_op jit(solution)/shard_map/march/pallas_call | solution.py:393
  45.6 6.0 %scale.1 = (f32[4,32,128,128]{3,2,1,0:T(8,128)}, f32[4,32,128,128]{3,2,1,0:T(8,128)}) custom-call(f32[6,34,128,128]{3,2,1,0:T(8,128)S(1)} %get-tuple-element.5.field, f32[4,32,128]{2,1,0:T(8,128)S(1)} %get-tuple-element.6.mean_ref, f32[4,32,128]{2,1,0:T(8,128)S(1)} %get-tuple-element.7.scale_ref), custom_call_target="tpu_custom_call" | custom-call | flops 4194304 | bytes 16777216 | tf_op jit(solution)/shard_map/scale/pallas_call | solution.py:432
